TPU v7x, 32 devices: a whole 2x2x4 slice. The times are simulated.
32 devices in a mesh: region: 2 (over x), leaf: 16 (over z, y, core).
Axes of the slice: x: 2, y: 2, z: 4, core: 2. Of those that a mesh axis runs over, the one named last changes fastest.
Arguments:
- whiten: bfloat16 [32, 1024, 1024], P(('region', 'leaf')), as said below
- leaf_root: bfloat16 [32, 1024, 512], P(('region', 'leaf')), may hold values from -6 to 6
- leaf_region: bfloat16 [32, 1024, 512], P(('region', 'leaf')), may hold values from -6 to 6
- root_factor: bfloat16 [512, 512], P('region'), may hold values from -0.25 to 0.25
- root_adjoint: bfloat16 [512, 512], P('region'), may hold values from -0.25 to 0.25
- region_factor: bfloat16 [2, 512, 512], P('region', 'leaf'), may hold values from -0.25 to 0.25
- region_adjoint: bfloat16 [2, 512, 512], P('region', 'leaf'), may hold values from -0.25 to 0.25
Outputs:
- grad_root_basis: bfloat16 [32, 1024, 512], P(('region', 'leaf'))
- grad_region_basis: bfloat16 [32, 1024, 512], P(('region', 'leaf'))
- grad_root_factor: float32 [512, 512], P('leaf')
- grad_region_factor: float32 [2, 512, 512], P('region', 'leaf')
Inputs may be any that keep to these rules, and one draw needn't show every extreme that they name: `whiten`: each whitening matrix is lower triangular with a positive diagonal.
All inputs are finite; a program needn't handle non-finite values.
Results may differ from a plain program's by a relative error of at most 0.018.
Values may be sent and summed in bfloat16 or wider, within the bound.
A program may use at most 64 MiB of HBM per device.

v0:
```python
import jax
import jax.numpy as jnp
from jax import lax
from jax.sharding import PartitionSpec as P


def on_device(
    whiten, leaf_root, leaf_region, root_factor, root_adjoint, region_factor, region_adjoint
):
    root_full, root_adj_full = (
        lax.all_gather(root_factor, "region", axis=0, tiled=True),
        lax.all_gather(root_adjoint, "region", axis=0, tiled=True),
    )
    region_full, region_adj_full = (
        lax.all_gather(region_factor, "leaf", axis=1, tiled=True),
        lax.all_gather(region_adjoint, "leaf", axis=1, tiled=True),
    )
    own_factor = region_full[0]
    own_adjoint = region_adj_full[0].astype(jnp.float32)
    root_wide = root_adj_full.astype(jnp.float32)
    root_sym = (root_wide + root_wide.T).astype(jnp.bfloat16)
    region_sym = (own_adjoint + own_adjoint.T).astype(jnp.bfloat16)
    root_basis = jnp.einsum(
        "lor,rk->lok", leaf_root, root_full, preferred_element_type=jnp.float32
    ).astype(jnp.bfloat16)
    region_basis = jnp.einsum(
        "lom,mk->lok", leaf_region, own_factor, preferred_element_type=jnp.float32
    ).astype(jnp.bfloat16)
    root_white = jnp.einsum(
        "lop,lpk->lok", whiten, root_basis, preferred_element_type=jnp.float32
    ).astype(jnp.bfloat16)
    region_white = jnp.einsum(
        "lop,lpk->lok", whiten, region_basis, preferred_element_type=jnp.float32
    ).astype(jnp.bfloat16)
    root_dwhite = jnp.einsum(
        "lok,kj->loj", root_white, root_sym, preferred_element_type=jnp.float32
    ).astype(jnp.bfloat16)
    region_dwhite = jnp.einsum(
        "lok,kj->loj", region_white, region_sym, preferred_element_type=jnp.float32
    ).astype(jnp.bfloat16)
    grad_root = jnp.einsum(
        "lpo,lpk->lok", whiten, root_dwhite, preferred_element_type=jnp.float32
    ).astype(jnp.bfloat16)
    grad_region = jnp.einsum(
        "lpo,lpk->lok", whiten, region_dwhite, preferred_element_type=jnp.float32
    ).astype(jnp.bfloat16)
    scale_obs = 1.0 / whiten.shape[1]
    root_term = (
        jnp.einsum("lor,lok->rk", leaf_root, grad_root, preferred_element_type=jnp.float32)
        * scale_obs
    )
    region_term = (
        jnp.einsum("lom,lok->mk", leaf_region, grad_region, preferred_element_type=jnp.float32)
        * scale_obs
    )
    region_part = lax.psum_scatter(
        region_term.astype(jnp.bfloat16), "leaf", scatter_dimension=0, tiled=True
    ).astype(jnp.float32)
    within = lax.psum_scatter(
        root_term.astype(jnp.bfloat16), "leaf", scatter_dimension=0, tiled=True
    )
    root_part = lax.psum(within, "region").astype(jnp.float32)
    return (grad_root, grad_region, root_part, region_part[None])


def solution(mesh):
    return jax.shard_map(
        on_device,
        mesh=mesh,
        in_specs=(
            P(("region", "leaf"), None, None),
            P(("region", "leaf"), None, None),
            P(("region", "leaf"), None, None),
            P("region", None),
            P("region", None),
            P("region", "leaf", None),
            P("region", "leaf", None),
        ),
        out_specs=(
            P(("region", "leaf"), None, None),
            P(("region", "leaf"), None, None),
            P("leaf", None),
            P("region", "leaf", None),
        ),
        check_vma=False,
    )
```

profile of v0, /device:TPU:0, one launch (start us, length us, event | category | flops | bytes accessed | tf_op | source)
XLA Modules:
  0.0 196.6 jit_solution(768296642538176674)
XLA Ops:
  7.2 0.0 copy-start
  7.2 0.0 copy-start.6
  7.2 0.0 reduce-scatter.9.cloned.1.call-start
  7.2 25.0 %all_gather.15 = bf16[1,512,512]{2,1,0:T(8,128)(2,1)S(1)} all-gather(bf16[1,32,512]{2,1,0:T(8,128)(2,1)} %param.13), channel_id=1, replica_groups=mesh['region'=2,'leaf'=16] {'leaf'}, dimensions={1}, use_global_device_ids=true | all-gather | bytes 557056 | tf_op jit(solution)/shard_map/all_gather | solution.py:16
  32.2 0.0 copy-start.1
  32.2 0.8 copy-done.1
  33.0 0.1 bitcast_convert_fusion
  33.1 1.3 copy.18
  34.4 0.0 copy-done.6
  34.4 18.9 %all_gather.14 = bf16[1,512,512]{2,1,0:T(8,128)(2,1)S(1)} all-gather(bf16[1,32,512]{2,1,0:T(8,128)(2,1)S(1)} %copy-done.6), channel_id=1, replica_groups=mesh['region'=2,'leaf'=16] {'leaf'}, dimensions={1}, use_global_device_ids=true | all-gather | bytes 557056 | tf_op jit(solution)/shard_map/all_gather | solution.py:15
  53.3 0.0 copy-done
  53.3 0.0 copy-start.2
  53.3 4.0 %fusion.14 = bf16[512,1024]{1,0:T(8,128)(2,1)} fusion(bf16[1,1024,1024]{2,1,0:T(8,128)(2,1)S(1)} %copy-done, bf16[1,1024,512]{2,1,0:T(8,128)(2,1)} %param.9, bf16[1,512,512]{2,1,0:T(8,128)(2,1)S(1)} %all_gather.14), kind=kOutput, calls=%fused_computation.10 | convolution fusion | flops 1611661312 | bytes 4718592 | tf_op jit(solution)/shard_map/lop,lpk->lok/dot_general | solution.py:32
  57.3 0.0 copy-done.2
  57.3 4.3 %fusion.17 = bf16[512,1024]{1,0:T(8,128)(2,1)} fusion(bf16[1,1024,1024]{2,1,0:T(8,128)(2,1)S(1)} %copy-done, bf16[512,1024]{1,0:T(8,128)(2,1)} %fusion.14, f32[512,512]{0,1:T(8,128)} %copy.18, bf16[1,512,512]{2,1,0:T(8,128)(2,1)S(1)} %copy-done.2), kind=kOutput, calls=%fused_computation.11 | convolution fusion | flops 1612447744 | bytes 5767168 | tf_op jit(solution)/shard_map/lpo,lpk->lok/dot_general | solution.py:44
  61.7 0.0 copy-start.4
  61.7 2.3 %fusion.22 = bf16[512,512]{0,1:T(8,128)(2,1)S(1)} fusion(bf16[512,1024]{1,0:T(8,128)(2,1)} %fusion.17, bf16[1,1024,512]{2,1,0:T(8,128)(2,1)} %param.9), kind=kOutput, calls=%fused_computation.20 | convolution fusion | flops 537395200 | bytes 2621440 | tf_op jit(solution)/shard_map/lom,lok->mk/dot_general | solution.py:53
  64.0 1.0 copy.25
  65.0 0.0 reduce-scatter.9.cloned.1.call-update
  65.0 0.0 reduce-scatter.7.cloned.1.call-start
  65.0 0.0 copy-done.4
  65.1 9.2 %all_gather.12 = bf16[512,512]{1,0:T(8,128)(2,1)S(1)} all-gather(bf16[256,512]{1,0:T(8,128)(2,1)S(1)} %copy-done.4), channel_id=1, replica_groups=mesh['region'=2,'leaf'=16] {'region'}, dimensions={0}, use_global_device_ids=true | all-gather | bytes 786432 | tf_op jit(solution)/shard_map/all_gather | solution.py:11
  74.3 0.0 copy-start.5
  74.3 4.0 %fusion.8 = bf16[512,1024]{1,0:T(8,128)(2,1)} fusion(bf16[1,1024,1024]{2,1,0:T(8,128)(2,1)S(1)} %copy-done, bf16[512,512]{1,0:T(8,128)(2,1)S(1)} %all_gather.12, bf16[1,1024,512]{2,1,0:T(8,128)(2,1)} %param.8), kind=kOutput, calls=%fused_computation.8 | convolution fusion | flops 1611661312 | bytes 4718592 | tf_op jit(solution)/shard_map/lop,lpk->lok/dot_general | solution.py:29
  78.3 0.0 copy-done.5
  78.3 8.3 %all_gather.13 = bf16[512,512]{1,0:T(8,128)(2,1)S(1)} all-gather(bf16[256,512]{1,0:T(8,128)(2,1)S(1)} %copy-done.5), channel_id=1, replica_groups=mesh['region'=2,'leaf'=16] {'region'}, dimensions={0}, use_global_device_ids=true | all-gather | bytes 786432 | tf_op jit(solution)/shard_map/all_gather | solution.py:12
  86.7 1.2 copy.17
  87.8 4.4 %fusion.11 = bf16[512,1024]{1,0:T(8,128)(2,1)} fusion(bf16[1,1024,1024]{2,1,0:T(8,128)(2,1)S(1)} %copy-done, bf16[512,1024]{1,0:T(8,128)(2,1)} %fusion.8, f32[512,512]{0,1:T(8,128)} %copy.17, bf16[512,512]{1,0:T(8,128)(2,1)S(1)} %all_gather.13), kind=kOutput, calls=%fused_computation.9 | convolution fusion | flops 1612447744 | bytes 5767168 | tf_op jit(solution)/shard_map/lpo,lpk->lok/dot_general | solution.py:41
  92.2 0.0 copy-start.3
  92.2 3.1 %fusion.23 = bf16[512,512]{0,1:T(8,128)(2,1)} fusion(bf16[512,1024]{1,0:T(8,128)(2,1)} %fusion.11, bf16[1,1024,512]{2,1,0:T(8,128)(2,1)} %param.8), kind=kOutput, calls=%fused_computation.21 | convolution fusion | flops 537395200 | bytes 2621440 | tf_op jit(solution)/shard_map/lor,lok->rk/dot_general | solution.py:49
  95.3 2.1 %copy.23 = bf16[512,512]{1,0:T(8,128)(2,1)} copy(bf16[512,512]{0,1:T(8,128)(2,1)} %fusion.23) | data formatting | bytes 1048576
  97.4 0.0 reduce-scatter.7.cloned.1.call-update
  97.4 0.0 copy-done.3
  97.4 1.3 copy.20
  98.8 2.3 %copy.19 = bf16[1,1024,512]{2,1,0:T(8,128)(2,1)} copy(bf16[1,1024,512]{1,2,0:T(8,128)(2,1)} %bitcast.75) | data formatting | bytes 2097152
  101.0 18.7 %reduce-scatter.9.cloned.1.call-done = bf16[32,512]{1,0:T(8,128)(2,1)} async-done(((bf16[512,512]{1,0:T(8,128)(2,1)}), bf16[32,512]{1,0:T(8,128)(2,1)}) %reduce-scatter.9.cloned.1.call-update) | async-done | bytes 32784
  119.7 0.9 copy.26
  120.6 0.7 copy.22
  121.4 57.2 %reduce-scatter.7.cloned.1.call-done = bf16[32,512]{1,0:T(8,128)(2,1)} async-done(((bf16[512,512]{1,0:T(8,128)(2,1)}), bf16[32,512]{1,0:T(8,128)(2,1)}) %reduce-scatter.7.cloned.1.call-update) | async-done | bytes 32784
  178.5 0.9 copy.24
  179.4 9.6 %psum.7 = bf16[32,512]{0,1:T(8,128)(2,1)S(1)} all-reduce(bf16[32,512]{0,1:T(8,128)(2,1)S(1)} %copy.24), channel_id=1, replica_groups=mesh['region'=2,'leaf'=16] {'region'}, use_global_device_ids=true, to_apply=%region_1.0 | all-reduce | flops 16384 | bytes 65536 | tf_op jit(solution)/shard_map/psum | solution.py:62
  189.0 0.7 copy.21
  (1 shorter events, 0.0 us)
Async XLA Ops:
  7.2 46.1 %copy-start = (bf16[1,1024,1024]{2,1,0:T(8,128)(2,1)S(1)}, bf16[1,1024,1024]{2,1,0:T(8,128)(2,1)}, u32[]{:S(2)}) copy-start(bf16[1,1024,1024]{2,1,0:T(8,128)(2,1)} %param.7) | copy-start | bytes 6291460
  7.2 27.2 %copy-start.6 = (bf16[1,32,512]{2,1,0:T(8,128)(2,1)S(1)}, bf16[1,32,512]{2,1,0:T(8,128)(2,1)}, u32[]{:S(2)}) copy-start(bf16[1,32,512]{2,1,0:T(8,128)(2,1)} %param.12) | copy-start | bytes 98308
  7.2 112.5 %reduce-scatter.9.cloned.1.call-start = ((), (), s32[]{:S(2)}) async-start(), calls=%async_computation.3 | async-start | bytes 557056
  32.2 0.8 copy-start.1
  53.3 4.0 %copy-start.2 = (bf16[1,512,512]{2,1,0:T(8,128)(2,1)S(1)}, bf16[1,512,512]{2,1,0:T(8,128)(2,1)}, u32[]{:S(2)}) copy-start(bf16[1,512,512]{2,1,0:T(8,128)(2,1)} %copy-done.1) | copy-start | bytes 1572868
  61.7 3.4 %copy-start.4 = (bf16[256,512]{1,0:T(8,128)(2,1)S(1)}, bf16[256,512]{1,0:T(8,128)(2,1)}, u32[]{:S(2)}) copy-start(bf16[256,512]{1,0:T(8,128)(2,1)} %param.10) | copy-start | bytes 786436
  65.0 113.6 %reduce-scatter.7.cloned.1.call-start = ((), (), s32[]{:S(2)}) async-start(), calls=%async_computation.2 | async-start | bytes 557056
  74.3 4.0 %copy-start.5 = (bf16[256,512]{1,0:T(8,128)(2,1)S(1)}, bf16[256,512]{1,0:T(8,128)(2,1)}, u32[]{:S(2)}) copy-start(bf16[256,512]{1,0:T(8,128)(2,1)} %param.11) | copy-start | bytes 786436
  92.2 5.2 %copy-start.3 = (bf16[512,1024]{1,0:T(8,128)(2,1)S(1)}, bf16[512,1024]{1,0:T(8,128)(2,1)}, u32[]{:S(2)}) copy-start(bf16[512,1024]{1,0:T(8,128)(2,1)} %fusion.17) | copy-start | bytes 3145732
Sparse Core Ops, SparseCore 0:
  65.1 54.5 reduce-scatter.8
  123.3 55.2 reduce-scatter.6
where the time goes:
time: 197 us
  waiting for transfers between devices  75.9 us (39%)
  blocking collectives  70.9 us (36%)
  matrix products  22.2 us (11%)
  between operations  14.1 us (7%)
  local copies, waits for them, and re-layouts  13.2 us (7%)
    unnamed x4, waiting for transfers between devices  75.9 us
    all_gather x1, blocking collectives, on_device(): lax.all_gather(region_adjoint, 'leaf', axis=1, tiled=True)  25 us
    all_gather x1, blocking collectives, on_device(): lax.all_gather(region_factor, 'leaf', axis=1, tiled=True)  18.9 us
    unnamed x22, local copies, waits for them, and re-layouts  10.7 us
    psum x1, blocking collectives, on_device(): root_part = lax.psum(within, 'region').astype(jnp.float32)  9.58 us
    all_gather x1, blocking collectives, on_device(): lax.all_gather(root_factor, 'region', axis=0, tiled=True)  9.22 us
    all_gather x1, blocking collectives, on_device(): lax.all_gather(root_adjoint, 'region', axis=0, tiled=True)  8.33 us
    dot_general x1, matrix products, on_device(): jnp.einsum('lpo,lpk->lok', whiten, root_dwhite, preferred_element_type=jn...  4.37 us
  transfers between devices with their start and end apart: 2, of which 2 were waited for; matrix products, arithmetic and copies ran while one was open for 10% of the time, Pallas kernels for 0%

commit v1 on v0

v1 whole, which is shorter than its diff:
```python
import functools
import math

import jax
import jax.numpy as jnp
from jax import lax
from jax.experimental import pallas as pl
from jax.experimental.pallas import tpu as pltpu
from jax.sharding import PartitionSpec as P

MESH = pl.DeviceIdType.MESH
F32, BF16 = jnp.float32, jnp.bfloat16


def split_leaf(leaves):
    chips = leaves // 2
    fast = max(d for d in range(1, math.isqrt(chips) + 1) if chips % d == 0)
    return chips // fast, fast


def dot(left, right):
    return jnp.dot(left, right, preferred_element_type=F32)


def kernel(
    nr, nl,
    w_in, lr_in, lg_in, rf_in, ra_in, gf_in, ga_in,
    gr_out, gg_out, fr_out, fg_out,
    w, l, a, b, rt, rg, g, grad, cb, rc, ys, ry, zs, rz, rx,
    ld, st, gz_s, gz_r, gy_s, gy_r, gc_s, gc_r, gx_s, gx_r, gp_s, gp_r,
    cs_s, cs_r, ys_s, ys_r, zs_s, zs_r, xs_s, xs_r,
):
    Z, Y = split_leaf(nl)
    obs, K = l.shape[1], l.shape[2]
    rows, half = K // nl, K // nr
    T = min(256, K)
    nb = obs // T
    r, leaf = lax.axis_index("region"), lax.axis_index("leaf")
    c, y, z = lax.rem(leaf, 2), lax.rem(leaf // 2, Y), leaf // (2 * Y)
    oc = 1 - c

    def at(zz, yy, cc):
        return (zz * Y + yy) * 2 + cc

    def zp(k):
        return lax.rem(z + k, Z)

    def zm(k):
        return lax.rem(z + Z - k, Z)

    def yp(k):
        return lax.rem(y + k, Y)

    def ym(k):
        return lax.rem(y + Y - k, Y)

    def rp(k):
        return lax.rem(r + k, nr)

    def rm(k):
        return lax.rem(r + nr - k, nr)

    def span(index, size):
        return pl.ds(pl.multiple_of(index * size, size), size)

    mine = span(leaf, rows)
    own = span(r, half)
    loads = [
        pltpu.make_async_copy(gf_in.at[0], rg.at[0, mine], ld.at[0]),
        pltpu.make_async_copy(ga_in.at[0], rg.at[1, mine], ld.at[1]),
        pltpu.make_async_copy(rf_in, rt.at[0, own], ld.at[2]),
        pltpu.make_async_copy(ra_in, rt.at[1, own], ld.at[3]),
        pltpu.make_async_copy(lr_in.at[0], l.at[0], ld.at[4]),
        pltpu.make_async_copy(w_in.at[0], w, ld.at[5]),
        pltpu.make_async_copy(lg_in.at[0], l.at[1], ld.at[6]),
    ]
    for load in loads:
        load.start()

    barrier = pltpu.get_barrier_semaphore()
    peers = [{"leaf": at(zp(k), y, c)} for k in range(1, Z)]
    peers += [{"leaf": at(z, yp(k), c)} for k in range(1, Y)]
    peers += [{"leaf": at(z, y, oc)}]
    peers += [{"region": rp(k)} for k in range(1, nr)]
    for peer in peers:
        pl.semaphore_signal(barrier, inc=1, device_id=peer, device_id_type=MESH)
    for load in loads[:4]:
        load.wait()
    pl.semaphore_wait(barrier, len(peers))

    sends = []

    def remote(src, dst, ssem, rsem, peer):
        return pltpu.make_async_remote_copy(
            src_ref=src, dst_ref=dst, send_sem=ssem, recv_sem=rsem,
            device_id=peer, device_id_type=MESH,
        )

    def send(src, dst, ssem, rsem, peer):
        copy = remote(src, dst, ssem, rsem, peer)
        copy.start()
        sends.append(copy)

    def arrive(ref, ssem, rsem, peer):
        remote(ref, ref, ssem, rsem, peer).wait_recv()

    other = {"leaf": at(z, y, oc)}

    def block(kz, ky, cc):
        return rg.at[:, span(at(zm(kz), ym(ky), cc), rows)]

    def gather_y(kz):
        for ky in range(1, Y):
            i = (ky - 1) * Z + kz
            send(block(kz, 0, c), block(kz, 0, c), gy_s.at[i], gy_r.at[i], {"leaf": at(z, yp(ky), c)})

    def gather_core(kz, ky):
        i = ky * Z + kz
        send(block(kz, ky, c), block(kz, ky, c), gc_s.at[i], gc_r.at[i], other)

    def z_forward(kz):
        arrive(block(kz, 0, c), gz_s.at[kz - 1], gz_r.at[kz - 1], other)
        gather_y(kz)
        gather_core(kz, 0)

    def y_forward(kz, ky):
        i = (ky - 1) * Z + kz
        arrive(block(kz, ky, c), gy_s.at[i], gy_r.at[i], other)
        gather_core(kz, ky)

    for k in range(1, Z):
        send(block(0, 0, c), block(0, 0, c), gz_s.at[k - 1], gz_r.at[k - 1], {"leaf": at(zp(k), y, c)})
    gather_y(0)
    for k in range(1, nr):
        send(rt.at[c, own], rt.at[c, own], gx_s.at[k - 1], gx_r.at[k - 1], {"region": rp(k)})
    gather_core(0, 0)

    scale = 1.0 / obs

    def local_a(p):
        for n in range(K // T):
            cols = pl.ds(n * T, T)
            for i in range(nb):
                a[p, pl.ds(i * T, T), cols] = dot(
                    w[pl.ds(i * T, T), pl.ds(0, (i + 1) * T)], l[p, pl.ds(0, (i + 1) * T), cols]
                ).astype(BF16)

    def local_c(p):
        per = T // (2 * Y * rows) if T >= 2 * Y * rows else 0
        step = T if per else 2 * Y * rows
        per = step // (2 * Y * rows)
        for i in range(K // step):
            left = a[p, :, pl.ds(i * step, step)].T
            part = (dot(left, a[p]) * scale).astype(BF16)
            cb[p, pl.ds(i * per, per)] = part.reshape(per, Y, 2, rows, K)
        send(cb.at[p, :, :, oc], rc.at[p], cs_s.at[p], cs_r.at[p], other)

    def local_b(i):
        left = w[pl.ds(i * T, obs - i * T), pl.ds(i * T, T)].T
        for p in range(2):
            b[p, pl.ds(i * T, T), :] = dot(left, a[p, pl.ds(i * T, obs - i * T), :]).astype(BF16)

    def reduce_y(p):
        arrive(rc.at[p], cs_s.at[p], cs_r.at[p], other)
        for k in range(1, Y):
            ys[p, k - 1] = (cb[p, :, yp(k), c].astype(F32) + rc[p, :, yp(k)].astype(F32)).astype(BF16)
            i = p * Y + k
            send(ys.at[p, k - 1], ry.at[p, k - 1], ys_s.at[i], ys_r.at[i], {"leaf": at(z, yp(k), c)})

    def chip_sum(p, zz):
        total = cb[p, zz, y, c].astype(F32) + rc[p, zz, y].astype(F32)
        for k in range(1, Y):
            total += ry[p, k - 1, zz].astype(F32)
        return total

    def reduce_z(p):
        for k in range(1, Y):
            i = p * Y + k
            arrive(ry.at[p, k - 1], ys_s.at[i], ys_r.at[i], other)
        for k in range(1, Z):
            zs[p, k - 1] = chip_sum(p, zp(k)).astype(BF16)
            i = p * Z + k
            send(zs.at[p, k - 1], rz.at[p, k - 1], zs_s.at[i], zs_r.at[i], {"leaf": at(zp(k), y, c)})

    def finish_z(p):
        total = chip_sum(p, z)
        for k in range(1, Z):
            i = p * Z + k
            arrive(rz.at[p, k - 1], zs_s.at[i], zs_r.at[i], other)
            total += rz[p, k - 1].astype(F32)
        return total

    def make_g(p, held):
        factor, adjoint = held[0], held[1]
        both = dot(factor, adjoint) + lax.dot_general(
            factor, adjoint, (((1,), (1,)), ((), ())), preferred_element_type=F32
        )
        g[p] = both.astype(BF16)

    def make_grad(p, out):
        for i in range(nb):
            grad[p, pl.ds(i * T, T), :] = dot(b[p, pl.ds(i * T, T), :], g[p]).astype(BF16)
        copy = pltpu.make_async_copy(grad.at[p], out.at[0], st.at[p])
        copy.start()
        return copy

    loads[4].wait()
    loads[5].wait()
    local_a(0)
    local_c(0)
    loads[6].wait()
    local_a(1)
    local_c(1)
    local_b(0)
    reduce_y(0)
    if Z > 1:
        z_forward(1)
    local_b(1)
    reduce_y(1)
    for k in range(2, Z):
        z_forward(k)
    for i in range(2, nb):
        local_b(i)
    for ky in range(1, Y):
        y_forward(0, ky)
    for k in range(1, nr):
        theirs = rt.at[c, span(rm(k), half)]
        arrive(theirs, gx_s.at[k - 1], gx_r.at[k - 1], other)
        send(theirs, theirs, gp_s.at[k - 1], gp_r.at[k - 1], other)
    reduce_z(0)
    for ky in range(1, Y):
        for k in range(1, Z):
            y_forward(k, ky)
    for k in range(1, nr):
        arrive(rt.at[oc, span(rm(k), half)], gp_s.at[k - 1], gp_r.at[k - 1], other)
    make_g(0, rt)
    store_root = make_grad(0, gr_out)
    reduce_z(1)
    rx[r] = finish_z(0).astype(BF16)
    for k in range(1, nr):
        send(rx.at[r], rx.at[r], xs_s.at[k - 1], xs_r.at[k - 1], {"region": rp(k)})
    for ky in range(Y):
        for kz in range(Z):
            i = ky * Z + kz
            arrive(block(kz, ky, oc), gc_s.at[i], gc_r.at[i], other)
    make_g(1, rg)
    store_region = make_grad(1, gg_out)
    fg_out[0] = dot(finish_z(1).astype(BF16), g[1])
    for k in range(1, nr):
        arrive(rx.at[rm(k)], xs_s.at[k - 1], xs_r.at[k - 1], other)
    total = rx[0].astype(F32)
    for k in range(1, nr):
        total += rx[k].astype(F32)
    fr_out[...] = dot(total.astype(BF16), g[0])
    store_root.wait()
    store_region.wait()
    for copy in sends:
        copy.wait_send()


def solution(mesh):
    nr, nl = mesh.shape["region"], mesh.shape["leaf"]
    Z, Y = split_leaf(nl)

    def on_device(whiten, leaf_root, leaf_region, root_factor, root_adjoint, region_factor, region_adjoint):
        obs, K = leaf_root.shape[1], leaf_root.shape[2]
        rows = K // nl
        dma = lambda n: pltpu.SemaphoreType.DMA((max(n, 1),))
        return pl.pallas_call(
            functools.partial(kernel, nr, nl),
            out_shape=(
                jax.ShapeDtypeStruct(leaf_root.shape, BF16),
                jax.ShapeDtypeStruct(leaf_region.shape, BF16),
                jax.ShapeDtypeStruct((rows, K), F32),
                jax.ShapeDtypeStruct((1, rows, K), F32),
            ),
            in_specs=[pl.BlockSpec(memory_space=pl.ANY)] * 7,
            out_specs=(
                pl.BlockSpec(memory_space=pl.ANY),
                pl.BlockSpec(memory_space=pl.ANY),
                pl.BlockSpec(memory_space=pltpu.VMEM),
                pl.BlockSpec(memory_space=pltpu.VMEM),
            ),
            scratch_shapes=[
                pltpu.VMEM((obs, obs), BF16),
                pltpu.VMEM((2, obs, K), BF16),
                pltpu.VMEM((2, obs, K), BF16),
                pltpu.VMEM((2, obs, K), BF16),
                pltpu.VMEM((2, K, K), BF16),
                pltpu.VMEM((2, K, K), BF16),
                pltpu.VMEM((2, K, K), BF16),
                pltpu.VMEM((2, obs, K), BF16),
                pltpu.VMEM((2, Z, Y, 2, rows, K), BF16),
                pltpu.VMEM((2, Z, Y, rows, K), BF16),
                pltpu.VMEM((2, max(Y - 1, 1), Z, rows, K), BF16),
                pltpu.VMEM((2, max(Y - 1, 1), Z, rows, K), BF16),
                pltpu.VMEM((2, max(Z - 1, 1), rows, K), BF16),
                pltpu.VMEM((2, max(Z - 1, 1), rows, K), BF16),
                pltpu.VMEM((nr, rows, K), BF16),
                dma(7), dma(2),
                dma(Z - 1), dma(Z - 1),
                dma((Y - 1) * Z), dma((Y - 1) * Z),
                dma(Y * Z), dma(Y * Z),
                dma(nr - 1), dma(nr - 1),
                dma(nr - 1), dma(nr - 1),
                dma(2), dma(2),
                dma(2 * Y), dma(2 * Y),
                dma(2 * Z), dma(2 * Z),
                dma(nr - 1), dma(nr - 1),
            ],
            compiler_params=pltpu.CompilerParams(
                collective_id=0, has_side_effects=True, vmem_limit_bytes=48 * 1024 * 1024
            ),
            name="likelihood_backward",
        )(whiten, leaf_root, leaf_region, root_factor, root_adjoint, region_factor, region_adjoint)

    return jax.shard_map(
        on_device,
        mesh=mesh,
        in_specs=(
            P(("region", "leaf"), None, None),
            P(("region", "leaf"), None, None),
            P(("region", "leaf"), None, None),
            P("region", None),
            P("region", None),
            P("region", "leaf", None),
            P("region", "leaf", None),
        ),
        out_specs=(
            P(("region", "leaf"), None, None),
            P(("region", "leaf"), None, None),
            P("leaf", None),
            P("region", "leaf", None),
        ),
        check_vma=False,
    )
```

time: 197 us -> 37.1 us (0.19)
  waiting for transfers between devices: 75.9 us -> 0 us
  blocking collectives: 70.9 us -> 0 us
  Pallas kernels: 0 us -> 27 us
  matrix products: 22.2 us -> 0 us
  between operations: 14.1 us -> 0.66 us
  local copies, waits for them, and re-layouts: 13.2 us -> 9.06 us
    unnamed x4 -> x0, waiting for transfers between devices: 75.9 us -> none
    all_gather x4 -> x0, blocking collectives: 61.4 us -> none  [the longest x1 25 us: on_device(): lax.all_gather(region_adjoint, 'leaf', axis=1, tiled=True)]
    pallas_call x0 -> x1, Pallas kernels: none -> 27 us  [on_device(): pl.pallas_call(functools.partial(kernel, nr, nl), out_shape=(jax.ShapeDty...]
    dot_general x6 -> x0, matrix products: 22.2 us -> none  [the longest x1 4.37 us: on_device(): jnp.einsum('lpo,lpk->lok', whiten, root_dwhite, preferred_element_type=jn...]
    psum x1 -> x0, blocking collectives: 9.58 us -> none  [on_device(): root_part = lax.psum(within, 'region').astype(jnp.float32)]
    convert_element_type x2 -> x0, local copies, waits for them, and re-layouts: 2.49 us -> none  [the longest x1 1.31 us: on_device(): own_adjoint = region_adj_full[0].astype(jnp.float32)]
    unnamed x22 -> x16, local copies, waits for them, and re-layouts: 10.7 us -> 9.06 us
  transfers between devices with their start and end apart: 2 -> 0, of which waited for: 2 -> 0; matrix products, arithmetic and copies ran while one was open for 10% -> 0% of each run, Pallas kernels for 0% -> 0%
where the time goes in v1:
time: 37.1 us; the launch traced here: 36.7 us
  Pallas kernels  27 us (73%)
  local copies, waits for them, and re-layouts  9.06 us (24%)
  between operations  0.66 us (2%)
    pallas_call x1, Pallas kernels, on_device(): pl.pallas_call(functools.partial(kernel, nr, nl), out_shape=(jax.ShapeDty...  27 us
    unnamed x16, local copies, waits for them, and re-layouts  9.06 us

profile of v1, /device:TPU:0, one launch (start us, length us, event | category | flops | bytes accessed | tf_op | source)
XLA Modules:
  0.0 36.7 jit_solution(14515555274779554819)
XLA Ops:
  0.6 0.0 copy-start
  0.6 1.2 %copy-done = bf16[1,1024,512]{2,1,0:T(8,128)(2,1)S(1)} copy-done((bf16[1,1024,512]{2,1,0:T(8,128)(2,1)S(1)}, bf16[1,1024,512]{2,1,0:T(8,128)(2,1)}, u32[]{:S(2)}) %copy-start) | copy-done | bytes 1048600
  1.9 0.0 copy-start.1
  1.9 1.2 %copy-done.1 = bf16[1,1024,512]{2,1,0:T(8,128)(2,1)S(1)} copy-done((bf16[1,1024,512]{2,1,0:T(8,128)(2,1)S(1)}, bf16[1,1024,512]{2,1,0:T(8,128)(2,1)}, u32[]{:S(2)}) %copy-start.1) | copy-done | bytes 1048600
  3.1 0.0 copy-start.2
  3.1 0.9 %copy-done.2 = bf16[256,512]{1,0:T(8,128)(2,1)S(1)} copy-done((bf16[256,512]{1,0:T(8,128)(2,1)S(1)}, bf16[256,512]{1,0:T(8,128)(2,1)}, u32[]{:S(2)}) %copy-start.2) | copy-done | bytes 262168
  4.0 0.0 copy-start.3
  4.0 0.9 %copy-done.3 = bf16[256,512]{1,0:T(8,128)(2,1)S(1)} copy-done((bf16[256,512]{1,0:T(8,128)(2,1)S(1)}, bf16[256,512]{1,0:T(8,128)(2,1)}, u32[]{:S(2)}) %copy-start.3) | copy-done | bytes 262168
  5.0 0.0 copy-start.4
  5.0 0.8 %copy-done.4 = bf16[1,32,512]{2,1,0:T(8,128)(2,1)S(1)} copy-done((bf16[1,32,512]{2,1,0:T(8,128)(2,1)S(1)}, bf16[1,32,512]{2,1,0:T(8,128)(2,1)}, u32[]{:S(2)}) %copy-start.4) | copy-done | bytes 32792
  5.7 0.0 copy-start.5
  5.7 0.8 %copy-done.5 = bf16[1,32,512]{2,1,0:T(8,128)(2,1)S(1)} copy-done((bf16[1,32,512]{2,1,0:T(8,128)(2,1)S(1)}, bf16[1,32,512]{2,1,0:T(8,128)(2,1)}, u32[]{:S(2)}) %copy-start.5) | copy-done | bytes 32792
  6.5 27.0 %likelihood_backward.1 = (bf16[1,1024,512]{2,1,0:T(8,128)(2,1)S(1)}, bf16[1,1024,512]{2,1,0:T(8,128)(2,1)S(1)}, f32[32,512]{1,0:T(8,128)S(1)}, f32[1,32,512]{2,1,0:T(8,128)S(1)}) custom-call(bf16[1,1024,1024]{2,1,0:T(8,128)(2,1)} %w_in.1, bf16[1,1024,512]{2,1,0:T(8,128)(2,1)S(1)} %copy-done, bf16[1,1024,512]{2,1,0:T(8,128)(2,1)S(1)} %copy-done.1, ...), custom_call_target="tpu_custom_call" | custom-call | tf_op jit(solution)/shard_map/likelihood_backward/pallas_call | solution.py:269
  33.5 1.0 %copy.15 = bf16[1,1024,512]{2,1,0:T(8,128)(2,1)} copy(bf16[1,1024,512]{2,1,0:T(8,128)(2,1)S(1)} %get-tuple-element.8) | data formatting | bytes 2097152
  34.4 1.0 %copy.16 = bf16[1,1024,512]{2,1,0:T(8,128)(2,1)} copy(bf16[1,1024,512]{2,1,0:T(8,128)(2,1)S(1)} %get-tuple-element.9) | data formatting | bytes 2097152
  35.4 0.6 %copy.17 = f32[32,512]{1,0:T(8,128)} copy(f32[32,512]{1,0:T(8,128)S(1)} %get-tuple-element.10) | data formatting | bytes 131072
  36.0 0.6 %copy.18 = f32[1,32,512]{2,1,0:T(8,128)} copy(f32[1,32,512]{2,1,0:T(8,128)S(1)} %get-tuple-element.11) | data formatting | bytes 131072
Async XLA Ops:
  0.6 1.2 %copy-start = (bf16[1,1024,512]{2,1,0:T(8,128)(2,1)S(1)}, bf16[1,1024,512]{2,1,0:T(8,128)(2,1)}, u32[]{:S(2)}) copy-start(bf16[1,1024,512]{2,1,0:T(8,128)(2,1)} %lr_in.1) | copy-start | bytes 3145732
  1.9 1.2 %copy-start.1 = (bf16[1,1024,512]{2,1,0:T(8,128)(2,1)S(1)}, bf16[1,1024,512]{2,1,0:T(8,128)(2,1)}, u32[]{:S(2)}) copy-start(bf16[1,1024,512]{2,1,0:T(8,128)(2,1)} %lg_in.1) | copy-start | bytes 3145732
  3.1 0.9 %copy-start.2 = (bf16[256,512]{1,0:T(8,128)(2,1)S(1)}, bf16[256,512]{1,0:T(8,128)(2,1)}, u32[]{:S(2)}) copy-start(bf16[256,512]{1,0:T(8,128)(2,1)} %rf_in.1) | copy-start | bytes 786436
  4.0 0.9 %copy-start.3 = (bf16[256,512]{1,0:T(8,128)(2,1)S(1)}, bf16[256,512]{1,0:T(8,128)(2,1)}, u32[]{:S(2)}) copy-start(bf16[256,512]{1,0:T(8,128)(2,1)} %ra_in.1) | copy-start | bytes 786436
  5.0 0.8 %copy-start.4 = (bf16[1,32,512]{2,1,0:T(8,128)(2,1)S(1)}, bf16[1,32,512]{2,1,0:T(8,128)(2,1)}, u32[]{:S(2)}) copy-start(bf16[1,32,512]{2,1,0:T(8,128)(2,1)} %gf_in.1) | copy-start | bytes 98308
  5.7 0.8 %copy-start.5 = (bf16[1,32,512]{2,1,0:T(8,128)(2,1)S(1)}, bf16[1,32,512]{2,1,0:T(8,128)(2,1)}, u32[]{:S(2)}) copy-start(bf16[1,32,512]{2,1,0:T(8,128)(2,1)} %ga_in.1) | copy-start | bytes 98308

commit v2 on v1

--- a/solution.py
+++ b/solution.py
@@ -16,6 +16,18 @@
     chips = leaves // 2
     fast = max(d for d in range(1, math.isqrt(chips) + 1) if chips % d == 0)
     return chips // fast, fast
+
+
+def offset(value, step, count):
+    if count & (count - 1):
+        return lax.rem(value + step, count), lax.rem(value + count - step, count)
+    bit = 1
+    pair = value
+    while bit < count:
+        if step & bit:
+            pair = pair + bit - 2 * bit * lax.rem(value // bit, 2)
+        bit *= 2
+    return pair, pair
 
 
 def dot(left, right):
@@ -43,16 +55,16 @@
         return (zz * Y + yy) * 2 + cc
 
     def zp(k):
-        return lax.rem(z + k, Z)
+        return offset(z, k, Z)[0]
 
     def zm(k):
-        return lax.rem(z + Z - k, Z)
+        return offset(z, k, Z)[1]
 
     def yp(k):
-        return lax.rem(y + k, Y)
+        return offset(y, k, Y)[0]
 
     def ym(k):
-        return lax.rem(y + Y - k, Y)
+        return offset(y, k, Y)[1]
 
     def rp(k):
         return lax.rem(r + k, nr)
@@ -160,30 +172,35 @@
         for p in range(2):
             b[p, pl.ds(i * T, T), :] = dot(left, a[p, pl.ds(i * T, obs - i * T), :]).astype(BF16)
 
+    far = range(Z - 1, -1, -1)
+
     def reduce_y(p):
         arrive(rc.at[p], cs_s.at[p], cs_r.at[p], other)
-        for k in range(1, Y):
-            ys[p, k - 1] = (cb[p, :, yp(k), c].astype(F32) + rc[p, :, yp(k)].astype(F32)).astype(BF16)
-            i = p * Y + k
-            send(ys.at[p, k - 1], ry.at[p, k - 1], ys_s.at[i], ys_r.at[i], {"leaf": at(z, yp(k), c)})
-
-    def chip_sum(p, zz):
+        for kz in far:
+            zz = zp(kz)
+            for k in range(1, Y):
+                yy = yp(k)
+                ys[p, k - 1, kz] = (cb[p, zz, yy, c].astype(F32) + rc[p, zz, yy].astype(F32)).astype(BF16)
+                i = (p * Y + k) * Z + kz
+                send(ys.at[p, k - 1, kz], ry.at[p, k - 1, kz], ys_s.at[i], ys_r.at[i], {"leaf": at(z, yy, c)})
+
+    def chip_sum(p, kz):
+        zz = zp(kz)
         total = cb[p, zz, y, c].astype(F32) + rc[p, zz, y].astype(F32)
         for k in range(1, Y):
-            total += ry[p, k - 1, zz].astype(F32)
+            i = (p * Y + k) * Z + kz
+            arrive(ry.at[p, k - 1, kz], ys_s.at[i], ys_r.at[i], other)
+            total += ry[p, k - 1, kz].astype(F32)
         return total
 
     def reduce_z(p):
-        for k in range(1, Y):
-            i = p * Y + k
-            arrive(ry.at[p, k - 1], ys_s.at[i], ys_r.at[i], other)
-        for k in range(1, Z):
-            zs[p, k - 1] = chip_sum(p, zp(k)).astype(BF16)
+        for k in far[:-1]:
+            zs[p, k - 1] = chip_sum(p, k).astype(BF16)
             i = p * Z + k
             send(zs.at[p, k - 1], rz.at[p, k - 1], zs_s.at[i], zs_r.at[i], {"leaf": at(zp(k), y, c)})
 
     def finish_z(p):
-        total = chip_sum(p, z)
+        total = chip_sum(p, 0)
         for k in range(1, Z):
             i = p * Z + k
             arrive(rz.at[p, k - 1], zs_s.at[i], zs_r.at[i], other)
@@ -199,7 +216,8 @@
 
     def make_grad(p, out):
         for i in range(nb):
-            grad[p, pl.ds(i * T, T), :] = dot(b[p, pl.ds(i * T, T), :], g[p]).astype(BF16)
+            part = pl.ds(i * T, T)
+            grad[p, part, :] = dot(b[p, part, :], g[p]).astype(BF16)
         copy = pltpu.make_async_copy(grad.at[p], out.at[0], st.at[p])
         copy.start()
         return copy
@@ -208,43 +226,44 @@
     loads[5].wait()
     local_a(0)
     local_c(0)
+    if Z > 1:
+        z_forward(1)
     loads[6].wait()
     local_a(1)
     local_c(1)
+    if Z > 2:
+        z_forward(2)
     local_b(0)
     reduce_y(0)
-    if Z > 1:
-        z_forward(1)
-    local_b(1)
+    for k in range(3, Z):
+        z_forward(k)
     reduce_y(1)
-    for k in range(2, Z):
-        z_forward(k)
-    for i in range(2, nb):
+    for i in range(1, nb):
         local_b(i)
     for ky in range(1, Y):
         y_forward(0, ky)
+    reduce_z(0)
     for k in range(1, nr):
         theirs = rt.at[c, span(rm(k), half)]
         arrive(theirs, gx_s.at[k - 1], gx_r.at[k - 1], other)
         send(theirs, theirs, gp_s.at[k - 1], gp_r.at[k - 1], other)
-    reduce_z(0)
     for ky in range(1, Y):
         for k in range(1, Z):
             y_forward(k, ky)
+    reduce_z(1)
     for k in range(1, nr):
         arrive(rt.at[oc, span(rm(k), half)], gp_s.at[k - 1], gp_r.at[k - 1], other)
     make_g(0, rt)
-    store_root = make_grad(0, gr_out)
-    reduce_z(1)
     rx[r] = finish_z(0).astype(BF16)
     for k in range(1, nr):
         send(rx.at[r], rx.at[r], xs_s.at[k - 1], xs_r.at[k - 1], {"region": rp(k)})
+    stores = [make_grad(0, gr_out)]
     for ky in range(Y):
         for kz in range(Z):
             i = ky * Z + kz
             arrive(block(kz, ky, oc), gc_s.at[i], gc_r.at[i], other)
     make_g(1, rg)
-    store_region = make_grad(1, gg_out)
+    stores.append(make_grad(1, gg_out))
     fg_out[0] = dot(finish_z(1).astype(BF16), g[1])
     for k in range(1, nr):
         arrive(rx.at[rm(k)], xs_s.at[k - 1], xs_r.at[k - 1], other)
@@ -252,10 +271,31 @@
     for k in range(1, nr):
         total += rx[k].astype(F32)
     fr_out[...] = dot(total.astype(BF16), g[0])
-    store_root.wait()
-    store_region.wait()
+    for copy in stores:
+        copy.wait()
     for copy in sends:
         copy.wait_send()
+
+
+def store(*refs):
+    source, target, held = refs[:4], refs[4:8], refs[8:12]
+    load_sem, store_sem = refs[12:]
+    pieces = []
+    for n in range(4):
+        extent = source[n].shape[-2]
+        size = min(extent, 256)
+        for row in range(0, extent, size):
+            where = (pl.ds(row, size),) if len(source[n].shape) == 2 else (0, pl.ds(row, size))
+            pieces.append((source[n].at[where], held[n].at[where], target[n].at[where]))
+    loads = [pltpu.make_async_copy(p[0], p[1], load_sem.at[i]) for i, p in enumerate(pieces)]
+    stores = [pltpu.make_async_copy(p[1], p[2], store_sem.at[i]) for i, p in enumerate(pieces)]
+    for load in loads:
+        load.start()
+    for load, save in zip(loads, stores):
+        load.wait()
+        save.start()
+    for save in stores:
+        save.wait()
 
 
 def solution(mesh):
@@ -266,7 +306,7 @@
         obs, K = leaf_root.shape[1], leaf_root.shape[2]
         rows = K // nl
         dma = lambda n: pltpu.SemaphoreType.DMA((max(n, 1),))
-        return pl.pallas_call(
+        held = pl.pallas_call(
             functools.partial(kernel, nr, nl),
             out_shape=(
                 jax.ShapeDtypeStruct(leaf_root.shape, BF16),
@@ -274,13 +314,8 @@
                 jax.ShapeDtypeStruct((rows, K), F32),
                 jax.ShapeDtypeStruct((1, rows, K), F32),
             ),
-            in_specs=[pl.BlockSpec(memory_space=pl.ANY)] * 7,
-            out_specs=(
-                pl.BlockSpec(memory_space=pl.ANY),
-                pl.BlockSpec(memory_space=pl.ANY),
-                pl.BlockSpec(memory_space=pltpu.VMEM),
-                pl.BlockSpec(memory_space=pltpu.VMEM),
-            ),
+            in_specs=[pl.BlockSpec(memory_space=pltpu.HBM)] * 7,
+            out_specs=(pl.BlockSpec(memory_space=pltpu.HBM),) * 2 + (pl.BlockSpec(memory_space=pltpu.VMEM),) * 2,
             scratch_shapes=[
                 pltpu.VMEM((obs, obs), BF16),
                 pltpu.VMEM((2, obs, K), BF16),
@@ -304,15 +339,24 @@
                 dma(nr - 1), dma(nr - 1),
                 dma(nr - 1), dma(nr - 1),
                 dma(2), dma(2),
-                dma(2 * Y), dma(2 * Y),
+                dma(2 * Y * Z), dma(2 * Y * Z),
                 dma(2 * Z), dma(2 * Z),
                 dma(nr - 1), dma(nr - 1),
             ],
             compiler_params=pltpu.CompilerParams(
-                collective_id=0, has_side_effects=True, vmem_limit_bytes=48 * 1024 * 1024
+                collective_id=0, has_side_effects=True, vmem_limit_bytes=67043328
             ),
             name="likelihood_backward",
         )(whiten, leaf_root, leaf_region, root_factor, root_adjoint, region_factor, region_adjoint)
+        return pl.pallas_call(
+            store,
+            out_shape=tuple(jax.ShapeDtypeStruct(x.shape, x.dtype) for x in held),
+            in_specs=[pl.BlockSpec(memory_space=pltpu.HBM)] * 4,
+            out_specs=(pl.BlockSpec(memory_space=pltpu.HBM),) * 4,
+            scratch_shapes=[pltpu.VMEM(x.shape, x.dtype) for x in held] + [dma(2 * pl.cdiv(obs, 256) + 2)] * 2,
+            compiler_params=pltpu.CompilerParams(vmem_limit_bytes=67043328),
+            name="store_outputs",
+        )(*held)
 
     return jax.shard_map(
         on_device,

time: 37.1 us -> 30 us (0.81)
  local copies, waits for them, and re-layouts: 9.06 us -> 0 us
  Pallas kernels: 27 us -> 29.2 us
    unnamed x16 -> x0, local copies, waits for them, and re-layouts: 9.06 us -> none
    pallas_call x0 -> x1, Pallas kernels: none -> 2.47 us  [on_device(): pl.pallas_call(store, out_shape=tuple((jax.ShapeDtypeStruct(x.shape, x.dt...]
where the time goes in v2:
time: 30 us; the launch traced here: 29.9 us
  Pallas kernels  29.2 us (97%)
  between operations  0.64 us (2%)
    pallas_call x1, Pallas kernels, on_device(): pl.pallas_call(functools.partial(kernel, nr, nl), out_shape=(jax.ShapeDty...  26.8 us
    pallas_call x1, Pallas kernels, on_device(): pl.pallas_call(store, out_shape=tuple((jax.ShapeDtypeStruct(x.shape, x.dt...  2.47 us

profile of v2, /device:TPU:0, one launch (start us, length us, event | category | flops | bytes accessed | tf_op | source)
XLA Modules:
  0.0 29.9 jit_solution(17237640964656871959)
XLA Ops:
  0.6 26.8 %likelihood_backward.1 = (bf16[1,1024,512]{2,1,0:T(8,128)(2,1)}, bf16[1,1024,512]{2,1,0:T(8,128)(2,1)}, f32[32,512]{1,0:T(8,128)}, f32[1,32,512]{2,1,0:T(8,128)}) custom-call(bf16[1,1024,1024]{2,1,0:T(8,128)(2,1)} %w_in.1, bf16[1,1024,512]{2,1,0:T(8,128)(2,1)} %lr_in.1, bf16[1,1024,512]{2,1,0:T(8,128)(2,1)} %lg_in.1, bf16[256,512]{1,0:T(8,128)(2,1)} %rf_in.1, ...), custom_call_target="tpu_custom_call" | custom-call | tf_op jit(solution)/shard_map/likelihood_backward/pallas_call | solution.py:309
  27.4 2.5 %store_outputs.1 = (bf16[1,1024,512]{2,1,0:T(8,128)(2,1)}, bf16[1,1024,512]{2,1,0:T(8,128)(2,1)}, f32[32,512]{1,0:T(8,128)}, f32[1,32,512]{2,1,0:T(8,128)}) custom-call(bf16[1,1024,512]{2,1,0:T(8,128)(2,1)} %get-tuple-element.8.refs_0_, bf16[1,1024,512]{2,1,0:T(8,128)(2,1)} %get-tuple-element.9.refs_1_, f32[32,512]{1,0:T(8,128)} %get-tuple-element.10.refs_2_, ...), custom_call_target="tpu_custom_call" | custom-call | tf_op jit(solution)/shard_map/store_outputs/pallas_call | solution.py:351
